TPU v7x, 32 devices: a whole 2x2x4 slice. The times are simulated.
32 devices in a mesh: grp: 4 (over y, x), brick: 8 (over z, core).
Axes of the slice: x: 2, y: 2, z: 4, core: 2. Of those that a mesh axis runs over, the one named last changes fastest.
Arguments:
- coeffs: bfloat16 [8, 4096, 1024], P(None, 'brick'), may hold values from -6 to 6
- tensor: bfloat16 [32, 1024, 1024], P('grp', 'brick'), may hold values from -0.005859375 to 0.005859375
- pairs: int32 [2, 2], replicated, may hold values from 0 to 7
- lateral: int32 [4096], P('brick'), may hold values from 0 to 511
- thermal: float32 [8], replicated, may hold values from 0.5 to 1
Outputs:
- updated: float32 [32, 8, 4096], P(None, None, 'brick')
Inputs may be any that keep to these rules, and one draw needn't show every extreme that they name: `pairs`: row p names the species that receives the collision term and the species it collides with. A cell's lateral partner, as an index within the same block of 512 cells.
All inputs are finite; a program needn't handle non-finite values.
Results may differ from a plain program's by a relative error of at most 0.0003.
Values may be sent and summed in bfloat16 or wider, within the bound.
A program may use at most 128 MiB of HBM per device.

v0:
```python
import jax
import jax.numpy as jnp
from jax import lax
from jax.sharding import PartitionSpec as P

PLANE = 128
collision_update = 0.5
courant = 0.08
max_speed = 11.0
mixing = 0.2


def with_halo(cells, sides, width):
    for axis, dim in sides:
        count = lax.axis_size(axis)
        head = lax.slice_in_dim(cells, 0, width, axis=dim)
        tail = lax.slice_in_dim(cells, cells.shape[dim] - width, cells.shape[dim], axis=dim)
        cells = jnp.concatenate(
            [
                lax.ppermute(tail, axis, [(i, (i + 1) % count) for i in range(count)]),
                cells,
                lax.ppermute(head, axis, [((i + 1) % count, i) for i in range(count)]),
            ],
            axis=dim,
        )
    return cells


def advance(extended, thermal, partner):
    mode_count = extended.shape[0] - 2
    thermo = thermal[None, :, None, None]
    orders = jnp.arange(mode_count, dtype=jnp.int32).astype(jnp.float32)[:, None, None, None]
    speed = thermo * (
        jnp.sqrt(orders) * extended[:mode_count] + jnp.sqrt(orders + 1.0) * extended[2:]
    )
    middle = extended[1 : mode_count + 1]
    face = 0.5 * (speed[:, :, :-1] + speed[:, :, 1:]) - 0.5 * max_speed * thermo * (
        middle[:, :, 1:] - middle[:, :, :-1]
    )
    center = middle[:, :, 1:-1]
    shape_flat = (mode_count, center.shape[1], center.shape[2] * center.shape[3])
    center = center.reshape(shape_flat)
    divergence = (face[:, :, 1:] - face[:, :, :-1]).reshape(shape_flat)
    beside = jnp.take(center, partner, axis=2)
    return center - courant * divergence + mixing * (beside - center)


def local(coeffs, tensor, pairs, lateral, thermal):
    species, cells, width = coeffs.shape
    local_modes = tensor.shape[0]
    group_count = lax.axis_size("grp")
    modes = local_modes * group_count
    pair_count = pairs.shape[0]
    layers = cells // PLANE
    left_rows = jnp.transpose(coeffs[pairs[:, 0]], (2, 0, 1))
    right_flat = coeffs[pairs[:, 1]].reshape(pair_count * cells, width)
    brick_window = jnp.transpose(coeffs[:, :, :modes], (2, 0, 1))
    padded_state = jnp.pad(brick_window, ((1, 1), (0, 0), (0, 0)))
    indicator_matrix = (
        pairs[:, 0][:, None] == jnp.arange(species, dtype=jnp.int32)[None, :]
    ).astype(jnp.float32)
    piece = lax.all_gather(tensor, "brick", axis=1, tiled=True)
    rows_here = piece.shape[1]
    inner = lax.dot_general(
        piece.reshape(local_modes * rows_here, width),
        right_flat,
        (((1,), (1,)), ((), ())),
        preferred_element_type=jnp.float32,
    )
    inner = inner.reshape(local_modes, rows_here, pair_count, cells)
    factor = left_rows.astype(jnp.float32)
    collide = jnp.sum(inner * factor[None], axis=1)
    pair_all = lax.all_gather(collide, "grp", axis=0, tiled=True)
    pair_extended = jnp.pad(pair_all, ((1, 1), (0, 0), (0, 0)))
    span = pair_extended.shape[0]
    collision_extended = jnp.einsum(
        "quw,ut->qtw", pair_extended, indicator_matrix, precision=lax.Precision.HIGHEST
    )
    species_state = padded_state.astype(jnp.float32) + collision_update * collision_extended
    extended = with_halo(species_state.reshape(span, species, layers, PLANE), (("brick", 2),), 1)
    updated = advance(extended, thermal, lateral)
    return updated


def solution(mesh):
    in_specs = (P(None, "brick", None), P("grp", "brick", None), P(), P("brick"), P())
    out_specs = P(None, None, "brick")
    return jax.shard_map(local, mesh=mesh, in_specs=in_specs, out_specs=out_specs, check_vma=False)
```

profile of v0, /device:TPU:0, one launch (start us, length us, event | category | flops | bytes accessed | tf_op | source)
XLA Modules:
  0.0 258.7 jit_solution(1344560839948286816)
XLA Ops:
  6.5 0.0 copy-start.2
  6.5 0.0 all-gather.2.cloned.1.call-start
  6.5 0.7 all-gather.2.cloned.1.call-update
  7.3 0.0 copy-done.2
  7.3 0.2 slice_reduce_fusion
  7.5 0.0 slice-start
  7.5 0.0 copy-start.3
  7.5 0.0 copy-start.1
  7.5 5.5 %gather_fusion = bf16[2,512,1024]{2,1,0:T(8,128)(2,1)} fusion(bf16[8,512,1024]{2,1,0:T(8,128)(2,1)} %param.5, s32[1024]{0:T(1024)S(1)} %get-tuple-element.11), kind=kCustom, calls=%fused_computation | custom fusion | bytes 4194312 | tf_op jit(solution)/shard_map/gather | solution.py:56
  13.0 4.1 %gather_fusion.1 = bf16[2,512,1024]{2,1,0:T(8,128)(2,1)S(1)} fusion(bf16[8,512,1024]{2,1,0:T(8,128)(2,1)} %param.5, s32[1024]{0:T(1024)S(1)} %get-tuple-element.10), kind=kCustom, calls=%fused_computation.1 | custom fusion | bytes 4194312 | tf_op jit(solution)/shard_map/gather | solution.py:55
  17.0 0.0 slice-done
  17.0 1.2 copy.14
  18.3 0.0 copy-done.3
  18.3 0.0 copy-done.1
  18.3 2.6 convert_bitcast_fusion
  20.9 141.9 %all-gather.2.cloned.1.call-done = bf16[8,1024,1024]{2,1,0:T(8,128)(2,1)} async-done(((bf16[8,128,1024]{2,1,0:T(8,128)(2,1)}), bf16[8,1024,1024]{2,1,0:T(8,128)(2,1)}) %all-gather.2.cloned.1.call-update) | async-done | bytes 16777232 | tf_op jit(solution)/shard_map/all_gather | solution.py:62
  162.8 25.8 %fusion.22 = f32[1024,8192]{1,0:T(8,128)} fusion(bf16[1024,1024]{1,0:T(8,128)(2,1)} %bitcast.38, bf16[8192,1024]{1,0:T(8,128)(2,1)} %bitcast.40), kind=kOutput, calls=%fused_computation.47 | convolution fusion | flops 17179869184 | bytes 52428800 | tf_op jit(solution)/shard_map/dot_general | solution.py:64
  188.6 0.0 copy-start
  188.6 37.4 %copy.15 = f32[128,8,8,1024]{3,2,1,0:T(8,128)S(1)} copy(f32[128,8,8,1024]{3,1,2,0:T(8,128)} %bitcast.34) | data formatting | bytes 67108864
  226.0 0.0 copy-done
  226.0 3.9 %multiply_reduce_fusion = f32[8,2,512]{0,2,1:T(8,128)S(1)} fusion(f32[8,1024,2,512]{1,0,3,2:T(8,128)S(1)} %bitcast.33, f32[1024,2,512]{0,2,1:T(8,128)S(1)} %copy-done), kind=kLoop, calls=%fused_computation.3 | loop fusion | flops 16769024 | bytes 37781504 | tf_op jit(solution)/shard_map/reduce_sum | solution.py:72
  230.0 0.2 copy.11
  230.1 8.4 %all_gather.7 = f32[32,2,512]{2,1,0:T(2,128)S(1)} all-gather(f32[8,2,512]{2,1,0:T(2,128)S(1)} %copy.11), channel_id=1, replica_groups=mesh['grp'=4,'brick'=8] {'grp'}, dimensions={0}, use_global_device_ids=true | all-gather | bytes 163840 | tf_op jit(solution)/shard_map/all_gather | solution.py:73
  238.6 1.5 fusion.1
  240.0 0.7 fusion.21
  240.8 0.0 collective-permute-start
  240.8 3.5 %collective-permute-start.1 = (f32[34,8,1,128]{3,1,2,0:T(8,128)}, f32[34,8,1,128]{3,1,2,0:T(8,128)S(1)}, u32[]{:S(2)}, u32[]{:S(2)}) collective-permute-start(f32[34,8,1,128]{3,1,2,0:T(8,128)} %get-tuple-element.8), channel_id=1, source_target_pairs={{1,0},{2,1},{3,2},{4,3},{5,4},{6,5},{7,6},{0,7},{9,8},{10,9},{11,1... | collective-permute-start | bytes 417800 | tf_op jit(solution)/shard_map/ppermute | solution.py:22
  244.4 0.8 copy.12
  245.2 2.7 %gather_fusion.2 = f32[512,32,8]{1,2,0:T(8,128)} fusion(f32[32,8,512]{0,1,2:T(8,128)S(1)} %copy.12, s32[1024]{0:T(1024)S(1)} %pad_clamp_fusion), kind=kCustom, calls=%fused_computation.2 | custom fusion | bytes 1050624 | tf_op jit(solution)/shard_map/jit(_take)/gather | solution.py:44
  247.9 2.4 copy.13
  250.3 0.0 collective-permute-done
  250.4 0.0 collective-permute-done.1
  250.4 0.1 pad_maximum_fusion
  250.4 0.2 fusion.3
  250.6 0.3 fusion.6
  250.9 1.0 fusion.11
  (7 shorter events, 0.1 us)
Async XLA Ops:
  6.5 0.7 copy-start.2
  6.5 156.2 %all-gather.2.cloned.1.call-start = ((), (), s32[]{:S(2)}) async-start(), calls=%async_computation | async-start | bytes 18874368 | tf_op jit(solution)/shard_map/all_gather | solution.py:62
  7.5 9.6 %slice-start = ((bf16[8,512,1024]{2,1,0:T(8,128)(2,1)}), bf16[8,512,32]{2,1,0:T(8,128)(2,1)S(1)}, s32[]{:S(2)}) async-start(bf16[8,512,1024]{2,1,0:T(8,128)(2,1)} %param.5), calls=%async_computation.1 | async-start | bytes 2097152 | tf_op jit(solution)/shard_map/slice | solution.py:57
  7.5 10.8 %copy-start.3 = (f32[8]{0:T(128)S(1)}, f32[8]{0:T(128)}, u32[]{:S(2)}) copy-start(f32[8]{0:T(128)} %param.9) | copy-start | bytes 100
  7.5 10.8 %copy-start.1 = (s32[512]{0:T(512)S(1)}, s32[512]{0:T(512)}, u32[]{:S(2)}) copy-start(s32[512]{0:T(512)} %param.8) | copy-start | bytes 6148
  188.6 37.4 %copy-start = (f32[1024,2,512]{0,2,1:T(8,128)S(1)}, f32[1024,2,512]{0,2,1:T(8,128)}, u32[]{:S(2)}) copy-start(f32[1024,2,512]{0,2,1:T(8,128)} %convert_bitcast_fusion) | copy-start | bytes 12582916
  240.8 9.6 %collective-permute-start = (f32[34,8,1,128]{3,1,2,0:T(8,128)}, f32[34,8,1,128]{3,1,2,0:T(8,128)S(1)}, u32[]{:S(2)}, u32[]{:S(2)}) collective-permute-start(f32[34,8,1,128]{3,1,2,0:T(8,128)} %get-tuple-element.9), channel_id=1, source_target_pairs={{0,1},{1,2},{2,3},{3,4},{4,5},{5,6},{6,7},{7,0},{8,9},{9,10},{10,1... | collective-permute-start | bytes 417800 | tf_op jit(solution)/shard_map/ppermute | solution.py:20
  240.8 9.6 %collective-permute-start.1 = (f32[34,8,1,128]{3,1,2,0:T(8,128)}, f32[34,8,1,128]{3,1,2,0:T(8,128)S(1)}, u32[]{:S(2)}, u32[]{:S(2)}) collective-permute-start(f32[34,8,1,128]{3,1,2,0:T(8,128)} %get-tuple-element.8), channel_id=1, source_target_pairs={{1,0},{2,1},{3,2},{4,3},{5,4},{6,5},{7,6},{0,7},{9,8},{10,9},{11,1... | collective-permute-start | bytes 417800 | tf_op jit(solution)/shard_map/ppermute | solution.py:22
Sparse Core Ops, SparseCore 0:
  8.9 153.7 all-gather.1
where the time goes:
time: 259 us
  waiting for transfers between devices  143 us (55%)
  local copies, waits for them, and re-layouts  55.1 us (21%)
  matrix products  27.3 us (11%)
  between operations  13.6 us (5%)
  blocking collectives  8.42 us (3%)
  other arithmetic  8.19 us (3%)
  starting transfers between devices  3.55 us (1%)
    all_gather x1, waiting for transfers between devices, local(): piece = lax.all_gather(tensor, 'brick', axis=1, tiled=True)  142 us
    unnamed x10, local copies, waits for them, and re-layouts  38.7 us
    dot_general x1, matrix products, local(): lax.dot_general(piece.reshape(local_modes * rows_here, width), right_flat...  25.8 us
    all_gather x1, blocking collectives, local(): pair_all = lax.all_gather(collide, 'grp', axis=0, tiled=True)  8.42 us
    gather x1, local copies, waits for them, and re-layouts, local(): right_flat = coeffs[pairs[:, 1]].reshape(pair_count * cells, width)  5.46 us
  transfers between devices with their start and end apart: 3, of which 1 were waited for; matrix products, arithmetic and copies ran while one was open for 8% of the time, Pallas kernels for 0%

commit v1 on v0

--- a/solution.py
+++ b/solution.py
@@ -59,7 +59,7 @@
     indicator_matrix = (
         pairs[:, 0][:, None] == jnp.arange(species, dtype=jnp.int32)[None, :]
     ).astype(jnp.float32)
-    piece = lax.all_gather(tensor, "brick", axis=1, tiled=True)
+    piece = jnp.concatenate(lax.all_gather(tensor, "brick"), axis=1)
     rows_here = piece.shape[1]
     inner = lax.dot_general(
         piece.reshape(local_modes * rows_here, width),

time: 259 us -> 272 us (1.050)
  local copies, waits for them, and re-layouts: 55.1 us -> 69.1 us
    reshape x0 -> x1, local copies, waits for them, and re-layouts: none -> 14 us  [local(): piece = jnp.concatenate(lax.all_gather(tensor, 'brick'), axis=1)]
    unnamed x10 -> x12, local copies, waits for them, and re-layouts: 38.7 us -> 38.7 us
  transfers between devices with their start and end apart: 3 -> 3, of which waited for: 1 -> 1; matrix products, arithmetic and copies ran while one was open for 8% -> 7% of each run, Pallas kernels for 0% -> 0%
where the time goes in v1:
time: 272 us
  waiting for transfers between devices  143 us (53%)
  local copies, waits for them, and re-layouts  69.1 us (25%)
  matrix products  26.6 us (10%)
  between operations  13.6 us (5%)
  blocking collectives  8.42 us (3%)
  other arithmetic  8.18 us (3%)
  starting transfers between devices  3.55 us (1%)
    all_gather x1, waiting for transfers between devices, local(): piece = jnp.concatenate(lax.all_gather(tensor, 'brick'), axis=1)  142 us
    unnamed x12, local copies, waits for them, and re-layouts  38.7 us
    dot_general x1, matrix products, local(): lax.dot_general(piece.reshape(local_modes * rows_here, width), right_flat...  25.1 us
    reshape x1, local copies, waits for them, and re-layouts, local(): piece = jnp.concatenate(lax.all_gather(tensor, 'brick'), axis=1)  14 us
    all_gather x1, blocking collectives, local(): pair_all = lax.all_gather(collide, 'grp', axis=0, tiled=True)  8.42 us
    gather x1, local copies, waits for them, and re-layouts, local(): right_flat = coeffs[pairs[:, 1]].reshape(pair_count * cells, width)  5.47 us
  transfers between devices with their start and end apart: 3, of which 1 were waited for; matrix products, arithmetic and copies ran while one was open for 7% of the time, Pallas kernels for 0%

profile of v1, /device:TPU:0, one launch (start us, length us, event | category | flops | bytes accessed | tf_op | source)
XLA Modules:
  0.0 272.0 jit_solution(11393871451394540053)
XLA Ops:
  6.5 0.0 copy-start.3
  6.5 0.0 all-gather.3.cloned.1.call-start
  6.5 0.7 all-gather.3.cloned.1.call-update
  7.3 0.0 copy-done.3
  7.3 0.2 slice_reduce_fusion
  7.5 0.0 slice-start
  7.5 0.0 copy-start.4
  7.5 0.0 copy-start.2
  7.5 5.5 %gather_fusion = bf16[2,512,1024]{2,1,0:T(8,128)(2,1)} fusion(bf16[8,512,1024]{2,1,0:T(8,128)(2,1)} %param.5, s32[1024]{0:T(1024)S(1)} %get-tuple-element.11), kind=kCustom, calls=%fused_computation | custom fusion | bytes 4194312 | tf_op jit(solution)/shard_map/gather | solution.py:56
  13.0 4.1 %gather_fusion.1 = bf16[2,512,1024]{2,1,0:T(8,128)(2,1)S(1)} fusion(bf16[8,512,1024]{2,1,0:T(8,128)(2,1)} %param.5, s32[1024]{0:T(1024)S(1)} %get-tuple-element.10), kind=kCustom, calls=%fused_computation.1 | custom fusion | bytes 4194312 | tf_op jit(solution)/shard_map/gather | solution.py:55
  17.0 0.0 slice-done
  17.0 1.2 copy.19
  18.3 0.0 copy-done.4
  18.3 0.0 copy-done.2
  18.3 2.6 convert_bitcast_fusion
  20.9 141.9 %all-gather.3.cloned.1.call-done = bf16[64,128,1024]{2,1,0:T(8,128)(2,1)} async-done(((bf16[8,128,1024]{2,1,0:T(8,128)(2,1)}), bf16[64,128,1024]{2,1,0:T(8,128)(2,1)}) %all-gather.3.cloned.1.call-update) | async-done | bytes 16777232 | tf_op jit(solution)/shard_map/all_gather | solution.py:62
  162.8 0.0 copy-start.1
  162.8 14.0 %copy.15 = bf16[8,8,128,1024]{3,2,1,0:T(8,128)(2,1)} copy(bf16[8,8,128,1024]{3,2,0,1:T(8,128)(2,1)} %bitcast.38) | data formatting | bytes 33554432 | tf_op jit(solution)/shard_map/reshape | solution.py:62
  176.8 0.0 copy-done.1
  176.8 25.1 %fusion.22 = f32[1024,8192]{1,0:T(8,128)} fusion(bf16[1024,1024]{1,0:T(8,128)(2,1)S(1)} %bitcast.43, bf16[8192,1024]{1,0:T(8,128)(2,1)} %bitcast.39), kind=kOutput, calls=%fused_computation.47 | convolution fusion | flops 17179869184 | bytes 52428800 | tf_op jit(solution)/shard_map/dot_general | solution.py:64
  201.9 0.0 copy-start
  201.9 37.4 %copy.20 = f32[128,8,8,1024]{3,2,1,0:T(8,128)S(1)} copy(f32[128,8,8,1024]{3,1,2,0:T(8,128)} %bitcast.37) | data formatting | bytes 67108864
  239.3 0.0 copy-done
  239.3 3.9 %multiply_reduce_fusion = f32[8,2,512]{0,2,1:T(8,128)S(1)} fusion(f32[8,1024,2,512]{1,0,3,2:T(8,128)S(1)} %bitcast.36, f32[1024,2,512]{0,2,1:T(8,128)S(1)} %copy-done), kind=kLoop, calls=%fused_computation.3 | loop fusion | flops 16769024 | bytes 37781504 | tf_op jit(solution)/shard_map/reduce_sum | solution.py:72
  243.3 0.2 copy.16
  243.4 8.4 %all_gather.11 = f32[32,2,512]{2,1,0:T(2,128)S(1)} all-gather(f32[8,2,512]{2,1,0:T(2,128)S(1)} %copy.16), channel_id=1, replica_groups=mesh['grp'=4,'brick'=8] {'grp'}, dimensions={0}, use_global_device_ids=true | all-gather | bytes 163840 | tf_op jit(solution)/shard_map/all_gather | solution.py:73
  251.9 1.5 fusion.1
  253.3 0.7 fusion.21
  254.1 0.0 collective-permute-start
  254.1 3.5 %collective-permute-start.1 = (f32[34,8,1,128]{3,1,2,0:T(8,128)}, f32[34,8,1,128]{3,1,2,0:T(8,128)S(1)}, u32[]{:S(2)}, u32[]{:S(2)}) collective-permute-start(f32[34,8,1,128]{3,1,2,0:T(8,128)} %get-tuple-element.8), channel_id=1, source_target_pairs={{1,0},{2,1},{3,2},{4,3},{5,4},{6,5},{7,6},{0,7},{9,8},{10,9},{11,1... | collective-permute-start | bytes 417800 | tf_op jit(solution)/shard_map/ppermute | solution.py:22
  257.7 0.8 copy.17
  258.5 2.7 %gather_fusion.2 = f32[512,32,8]{1,2,0:T(8,128)} fusion(f32[32,8,512]{0,1,2:T(8,128)S(1)} %copy.17, s32[1024]{0:T(1024)S(1)} %pad_clamp_fusion), kind=kCustom, calls=%fused_computation.2 | custom fusion | bytes 1050624 | tf_op jit(solution)/shard_map/jit(_take)/gather | solution.py:44
  261.2 2.4 copy.18
  263.6 0.0 collective-permute-done
  263.7 0.0 collective-permute-done.1
  263.7 0.1 pad_maximum_fusion
  263.7 0.2 fusion.3
  263.9 0.3 fusion.6
  264.2 1.0 fusion.11
  (7 shorter events, 0.1 us)
Async XLA Ops:
  6.5 0.7 copy-start.3
  6.5 156.2 %all-gather.3.cloned.1.call-start = ((), (), s32[]{:S(2)}) async-start(), calls=%async_computation | async-start | bytes 18874368 | tf_op jit(solution)/shard_map/all_gather | solution.py:62
  7.5 9.6 %slice-start = ((bf16[8,512,1024]{2,1,0:T(8,128)(2,1)}), bf16[8,512,32]{2,1,0:T(8,128)(2,1)S(1)}, s32[]{:S(2)}) async-start(bf16[8,512,1024]{2,1,0:T(8,128)(2,1)} %param.5), calls=%async_computation.1 | async-start | bytes 2097152 | tf_op jit(solution)/shard_map/slice | solution.py:57
  7.5 10.8 %copy-start.4 = (f32[8]{0:T(128)S(1)}, f32[8]{0:T(128)}, u32[]{:S(2)}) copy-start(f32[8]{0:T(128)} %param.9) | copy-start | bytes 100
  7.5 10.8 %copy-start.2 = (s32[512]{0:T(512)S(1)}, s32[512]{0:T(512)}, u32[]{:S(2)}) copy-start(s32[512]{0:T(512)} %param.8) | copy-start | bytes 6148
  162.8 14.0 %copy-start.1 = (bf16[2,512,1024]{2,1,0:T(8,128)(2,1)S(1)}, bf16[2,512,1024]{2,1,0:T(8,128)(2,1)}, u32[]{:S(2)}) copy-start(bf16[2,512,1024]{2,1,0:T(8,128)(2,1)} %gather_fusion) | copy-start | bytes 6291460
  201.9 37.4 %copy-start = (f32[1024,2,512]{0,2,1:T(8,128)S(1)}, f32[1024,2,512]{0,2,1:T(8,128)}, u32[]{:S(2)}) copy-start(f32[1024,2,512]{0,2,1:T(8,128)} %convert_bitcast_fusion) | copy-start | bytes 12582916
  254.1 9.6 %collective-permute-start = (f32[34,8,1,128]{3,1,2,0:T(8,128)}, f32[34,8,1,128]{3,1,2,0:T(8,128)S(1)}, u32[]{:S(2)}, u32[]{:S(2)}) collective-permute-start(f32[34,8,1,128]{3,1,2,0:T(8,128)} %get-tuple-element.9), channel_id=1, source_target_pairs={{0,1},{1,2},{2,3},{3,4},{4,5},{5,6},{6,7},{7,0},{8,9},{9,10},{10,1... | collective-permute-start | bytes 417800 | tf_op jit(solution)/shard_map/ppermute | solution.py:20
  254.1 9.6 %collective-permute-start.1 = (f32[34,8,1,128]{3,1,2,0:T(8,128)}, f32[34,8,1,128]{3,1,2,0:T(8,128)S(1)}, u32[]{:S(2)}, u32[]{:S(2)}) collective-permute-start(f32[34,8,1,128]{3,1,2,0:T(8,128)} %get-tuple-element.8), channel_id=1, source_target_pairs={{1,0},{2,1},{3,2},{4,3},{5,4},{6,5},{7,6},{0,7},{9,8},{10,9},{11,1... | collective-permute-start | bytes 417800 | tf_op jit(solution)/shard_map/ppermute | solution.py:22
Sparse Core Ops, SparseCore 0:
  8.9 153.7 all-gather.2
